TPU v7x, 32 devices: a whole 2x2x4 slice. The times are simulated.
32 devices in a mesh: dp: 2 (over x), fsdp: 4 (over y, core), tensor: 4 (over z).
Axes of the slice: x: 2, y: 2, z: 4, core: 2. Of those that a mesh axis runs over, the one named last changes fastest.
Arguments:
- hidden: bfloat16 [4096, 2048], P(('dp', 'fsdp'), 'tensor'), may hold values from -8 to 8
- norm_gain: bfloat16 [2048], P('tensor'), may hold values from 0.099609375 to 1.8984375
- head_weight: bfloat16 [2048, 32128], P('fsdp', 'tensor'), may hold values from -1 to 1
- token_ids: int32 [8, 512], P(('dp', 'fsdp')), may hold values from 0 to 32127
- lengths: int32 [8], P(('dp', 'fsdp')), may hold values from 128 to 512
- old_logp: float32 [8, 512], P(('dp', 'fsdp')), may hold values from -12.5 to -9.5
- advantages: float32 [8, 512], P(('dp', 'fsdp')), may hold values from -4 to 4
- rollout_logp: float32 [8, 512], P(('dp', 'fsdp'), 'tensor'), may hold values from -16 to -1
- rollout_row: int32 [8], P(('dp', 'fsdp')), may hold values from 0 to 7, each once
Outputs:
- new_logp: float32 [8, 512], P(('dp', 'fsdp'))
- token_loss: float32 [8, 512], P(('dp', 'fsdp'))
- summary: float32 [3], replicated
Inputs may be any that keep to these rules, and one draw needn't show every extreme that they name: `rollout_row`: every row 0 to 7 is named once.
All inputs are finite; a program needn't handle non-finite values.
Results may differ from a plain program's by a relative error of at most 0.0005.
The roundings to bfloat16 on the way count: a program that leaves them out, or rounds other values in their place, can miss the bound.
Values may be sent and summed in bfloat16 or wider, within the bound.
A program may use at most 128 MiB of HBM per device.

v0:
```python
import jax
import jax.numpy as jnp
from jax import lax
from jax.sharding import PartitionSpec as P

clip_eps = 0.2
kl_coef = 0.2
log_limit = 10.0
norm_eps = 1e-06


def combined_all(value, axis, join):
    pieces = jax.tree.map(lambda part: lax.all_gather(part, axis), value)
    head = jax.tree.map(lambda part: part[0], pieces)
    tail = jax.tree.map(lambda part: part[1:], pieces)
    so_far, _ = lax.scan(lambda so_far, section: (join(so_far, section), None), head, tail)
    return so_far


def token_terms(new_logp, old_logp, advantages, ref_logp, live_mask, prob_square):
    shift = new_logp - old_logp
    prob_ratio = jnp.exp(jnp.clip(shift, -log_limit, log_limit))
    clipped = jnp.clip(prob_ratio, 1.0 - clip_eps, 1.0 + clip_eps)
    plain_term = prob_ratio * advantages
    bounded_term = clipped * advantages
    surrogate = jnp.minimum(plain_term, bounded_term)
    ref_gap = ref_logp - new_logp
    gap_clip = jnp.clip(ref_gap, -log_limit, log_limit)
    kl_term = jnp.exp(gap_clip) - gap_clip - 1.0
    token_loss = live_mask * (kl_coef * kl_term - surrogate)
    inside_gap = (jnp.abs(ref_gap) < log_limit).astype(jnp.float32)
    inside_ratio = (jnp.abs(shift) < log_limit).astype(jnp.float32)
    active_term = (plain_term <= bounded_term).astype(jnp.float32)
    grad_coef = live_mask * (
        kl_coef * (1.0 - jnp.exp(gap_clip)) * inside_gap
        - advantages * prob_ratio * active_term * inside_ratio
    )
    grad_square = grad_coef * grad_coef * (prob_square - 2.0 * jnp.exp(new_logp) + 1.0)
    return (token_loss, live_mask * kl_term, grad_square)


def join_stats(earlier, later):
    row_max = jnp.maximum(earlier[0], later[0])
    left_scale = jnp.exp(earlier[0] - row_max)
    right_scale = jnp.exp(later[0] - row_max)
    exp_sum = earlier[1] * left_scale + later[1] * right_scale
    exp_square = earlier[2] * left_scale * left_scale + later[2] * right_scale * right_scale
    return (row_max, exp_sum, exp_square, earlier[3] + later[3])


def exp_sums(logits, row_max):
    shifted = jnp.exp(logits - row_max[:, None])
    return (jnp.sum(shifted, axis=1), jnp.sum(shifted * shifted, axis=1))


def vocab_stats(logits, flat_ids, col_start):
    col_ids = lax.broadcasted_iota(jnp.int32, logits.shape, 1) + col_start
    picked = jnp.sum(jnp.where(col_ids == flat_ids[:, None], logits, 0.0), axis=1)
    local_max = jnp.max(logits, axis=1)
    row_max = lax.pmax(local_max, "tensor")
    exp_sum, exp_square = exp_sums(logits, row_max)
    exp_sum, exp_square, picked = lax.psum((exp_sum, exp_square, picked), "tensor")
    return (row_max, exp_sum, exp_square, picked)


def shards(
    hidden,
    norm_gain,
    head_weight,
    token_ids,
    lengths,
    old_logp,
    advantages,
    rollout_logp,
    rollout_row,
):
    tok_rows = hidden.shape[0]
    full_rows, full_gain = (
        lax.all_gather(hidden, "tensor", axis=1, tiled=True),
        lax.all_gather(norm_gain, "tensor", axis=0, tiled=True),
    )
    values = full_rows.astype(jnp.float32)
    inv_rms = lax.rsqrt(jnp.mean(values * values, axis=1, keepdims=True) + norm_eps)
    normed = (values * inv_rms * full_gain.astype(jnp.float32)[None, :]).astype(jnp.bfloat16)
    flat_ids = token_ids.reshape(-1)
    vocab_cols = head_weight.shape[1]
    tensor_pos = lax.axis_index("tensor")
    half_cols = vocab_cols // 2
    dp_pos = lax.axis_index("dp")
    own_cols = lax.dynamic_slice_in_dim(head_weight, dp_pos * half_cols, half_cols, 1)
    pair_rows = lax.all_gather(normed, "dp", axis=0, tiled=True)
    pair_ids = lax.all_gather(flat_ids, "dp", axis=0, tiled=True)
    logits = jnp.dot(
        pair_rows,
        lax.all_gather(own_cols, "fsdp", axis=0, tiled=True),
        preferred_element_type=jnp.float32,
    )
    soft_stats = vocab_stats(logits, pair_ids, tensor_pos * vocab_cols + dp_pos * half_cols)
    soft_stats = combined_all(soft_stats, "dp", join_stats)
    soft_stats = tuple(
        (lax.dynamic_slice_in_dim(member, dp_pos * tok_rows, tok_rows, 0) for member in soft_stats)
    )
    row_max, exp_sum, exp_square, picked = soft_stats
    new_logp = (picked - row_max - jnp.log(exp_sum)).reshape(token_ids.shape)
    prob_square = (exp_square / (exp_sum * exp_sum)).reshape(token_ids.shape)
    ref_all = lax.all_gather(rollout_logp, ("dp", "fsdp"), axis=0, tiled=True)
    own_ref = jnp.take(ref_all, rollout_row, axis=0)
    ref_logp = lax.all_gather(own_ref, "tensor", axis=1, tiled=True)
    positions = lax.broadcasted_iota(jnp.int32, token_ids.shape, 1)
    live_mask = (positions < lengths[:, None]).astype(jnp.float32)
    token_loss, kl_part, grad_part = token_terms(
        new_logp, old_logp, advantages, ref_logp, live_mask, prob_square
    )
    live_count, loss_sum, kl_sum, grad_sum = lax.psum(
        (jnp.sum(live_mask), jnp.sum(token_loss), jnp.sum(kl_part), jnp.sum(grad_part)),
        ("dp", "fsdp"),
    )
    summary = jnp.stack(
        [loss_sum / live_count, kl_sum / live_count, jnp.sqrt(grad_sum / live_count)]
    )
    return (new_logp, token_loss, summary)


def solution(mesh):
    in_specs = (
        P(("dp", "fsdp"), "tensor"),
        P("tensor"),
        P("fsdp", "tensor"),
        P(("dp", "fsdp"), None),
        P(("dp", "fsdp")),
        P(("dp", "fsdp"), None),
        P(("dp", "fsdp"), None),
        P(("dp", "fsdp"), "tensor"),
        P(("dp", "fsdp")),
    )
    out_specs = (P(("dp", "fsdp"), None), P(("dp", "fsdp"), None), P())
    return jax.shard_map(shards, mesh=mesh, in_specs=in_specs, out_specs=out_specs, check_vma=False)
```

profile of v0, /device:TPU:0, one launch (start us, length us, event | category | flops | bytes accessed | tf_op | source)
XLA Modules:
  0.0 327.2 jit_solution(12771580866404278968)
XLA Ops:
  7.2 0.0 all-gather.11.cloned.1.call-start
  7.2 0.7 all-gather.11.cloned.1.call-update
  7.9 0.0 all-gather.13.cloned.1.call-start
  7.9 0.7 reshape.90
  8.6 13.6 %all-gather.2 = bf16[4,1,512]{2,1,0:T(2,128)(2,1)S(1)} all-gather(bf16[1,1,512]{2,1,0:T(2,128)(2,1)S(1)} %reshape.90), channel_id=1, replica_groups=mesh['dp'=2,'fsdp'=4,'tensor'=4] {'tensor'}, dimensions={0}, use_global_device_ids=true | all-gather | bytes 5120 | tf_op jit(solution)/shard_map/all_gather | solution.py:80
  22.3 35.7 %all-gather.11.cloned.1.call-done = bf16[512,2048]{1,0:T(8,128)(2,1)} async-done(((bf16[512,512]{1,0:T(8,128)(2,1)}), bf16[512,2048]{1,0:T(8,128)(2,1)}) %all-gather.11.cloned.1.call-update) | async-done | bytes 2097168 | tf_op jit(solution)/shard_map/all_gather | solution.py:79
  58.0 2.1 fusion.1
  60.0 3.5 %fusion.3 = bf16[512,2048]{1,0:T(8,128)(2,1)} fusion(bf16[512,2048]{1,0:T(8,128)(2,1)} %all-gather.11.cloned.1.call-done, f32[2048]{0:T(1024)S(1)} %bitcast.29, f32[512]{0:T(512)S(1)} %add_rsqrt_fusion), kind=kLoop, calls=%fused_computation.8 | loop fusion | flops 4194304 | bytes 4204544 | tf_op jit(solution)/shard_map/convert_element_type | solution.py:84
  63.5 0.0 all-gather.13.cloned.1.call-update
  63.5 0.0 all-gather.15.cloned.1.call-start
  63.6 0.0 copy-start.1
  63.6 4.4 %constant_dynamic-slice_fusion.1 = bf16[512,4016]{0,1:T(8,128)(2,1)} fusion(bf16[512,8032]{0,1:T(8,128)(2,1)} %param.11, s32[]{:T(128)S(6)} %select_n.30), kind=kLoop, calls=%fused_computation.37 | loop fusion | bytes 8224772 | tf_op jit(solution)/shard_map/dynamic_slice | solution.py:90
  68.0 0.0 all-gather.15.cloned.1.call-update
  69.3 0.6 convert_reduce_fusion
  70.0 8.9 %all-gather.5 = f32[8,1,128]{2,1,0:T(1,128)S(1)} all-gather(f32[1,1,128]{2,1,0:T(1,128)S(1)} %bitcast.45), channel_id=1, replica_groups=mesh['dp'=2,'fsdp'=4,'tensor'=4] {'dp','fsdp'}, dimensions={0}, use_global_device_ids=true | all-gather | bytes 4608 | tf_op jit(solution)/shard_map/all_gather | solution.py:106
  78.8 8.6 %all_gather.57 = f32[1,512]{1,0:T(1,128)S(1)} all-gather(f32[1,128]{1,0:T(1,128)S(1)} %fusion.8), channel_id=1, replica_groups=mesh['dp'=2,'fsdp'=4,'tensor'=4] {'tensor'}, dimensions={1}, use_global_device_ids=true | all-gather | bytes 2560 | tf_op jit(solution)/shard_map/all_gather | solution.py:108
  87.4 4.5 %all-gather = s32[1,1024]{1,0:T(1,128)S(1)} all-gather(s32[1,512]{1,0:T(1,128)S(1)} %copy-done.1), channel_id=2, replica_groups=mesh['dp'=2,'fsdp'=4,'tensor'=4] {'dp'}, dimensions={1}, use_global_device_ids=true | all-gather | bytes 6144 | tf_op jit(solution)/shard_map/all_gather | solution.py:92
  92.0 27.3 %all-gather.13.cloned.1.call-done = bf16[1024,2048]{1,0:T(8,128)(2,1)} async-done(((bf16[512,2048]{1,0:T(8,128)(2,1)}), bf16[1024,2048]{1,0:T(8,128)(2,1)}) %all-gather.13.cloned.1.call-update) | async-done | bytes 4194320 | tf_op jit(solution)/shard_map/all_gather | solution.py:91
  119.3 105.6 %all-gather.15.cloned.1.call-done = bf16[2048,4016]{0,1:T(8,128)(2,1)} async-done(((bf16[512,4016]{0,1:T(8,128)(2,1)}), bf16[2048,4016]{0,1:T(8,128)(2,1)}) %all-gather.15.cloned.1.call-update) | async-done | bytes 16449552 | tf_op jit(solution)/shard_map/all_gather | solution.py:95
  224.9 23.4 %fusion.15 = (f32[1024]{0:T(1024)S(1)}, f32[1024,4016]{0,1:T(8,128)}) fusion(bf16[1024,2048]{1,0:T(8,128)(2,1)} %all-gather.13.cloned.1.call-done, bf16[2048,4016]{0,1:T(8,128)(2,1)} %all-gather.15.cloned.1.call-done), kind=kOutput, calls=%fused_computation.46 | convolution fusion | flops 16848436224 | bytes 37097472 | tf_op jit(solution)/shard_map/dot_general | solution.py:93
  248.3 11.7 %pmax.7 = f32[1024]{0:T(1024)S(1)} all-reduce(f32[1024]{0:T(1024)S(1)} %get-tuple-element.65), channel_id=1, replica_groups=mesh['dp'=2,'fsdp'=4,'tensor'=4] {'tensor'}, use_global_device_ids=true, to_apply=%region_4.5 | all-reduce | flops 1024 | bytes 8192 | tf_op jit(solution)/shard_map/pmax | solution.py:60
  259.9 4.3 %all-gather.1 = f32[2048]{0:T(1024)S(1)} all-gather(f32[1024]{0:T(1024)S(1)} %pmax.7), channel_id=3, replica_groups=mesh['dp'=2,'fsdp'=4,'tensor'=4] {'dp'}, dimensions={0}, use_global_device_ids=true | all-gather | bytes 12288 | tf_op jit(solution)/shard_map/all_gather | solution.py:13
  264.3 8.7 %multiply_reduce_fusion = (f32[1024]{0:T(1024)S(1)}, f32[1024]{0:T(1024)S(1)}, f32[1024]{0:T(1024)S(1)}) fusion(f32[1024,4016]{0,1:T(8,128)} %get-tuple-element.66, f32[1024]{0:T(1024)S(1)} %pmax.7, s32[1024]{0:T(1024)S(1)} %bitcast.33, s32[4016]{0:T(1024)S(1)} %iota_add_fusion), kind=kLoop, calls=%fused_computation | loop fusion | flops 28783616 | bytes 16486080 | tf_op jit(solution)/shard_map/reduce_sum | solution.py:53
  273.0 15.5 %all-reduce.1 = (f32[1,1024]{1,0:T(1,128)S(1)}, f32[1,1024]{1,0:T(1,128)S(1)}, f32[1,1024]{1,0:T(1,128)S(1)}) all-reduce(f32[1,1024]{1,0:T(1,128)S(1)} %bitcast.32, f32[1,1024]{1,0:T(1,128)S(1)} %bitcast.31, f32[1,1024]{1,0:T(1,128)S(1)} %bitcast.30), channel_id=1, replica_groups=mesh['dp'=2,'fsdp'=4,'tensor'=4] {'tensor'}, use_global_device_ids=true, to_apply=%region_2.3 | all-reduce | flops 3072 | bytes 24576 | tf_op jit(solution)/shard_map/psum | solution.py:62
  288.5 4.3 %all-gather.3 = f32[2,1,1024]{2,1,0:T(1,128)S(1)} all-gather(f32[1,1,1024]{2,1,0:T(1,128)S(1)} %bitcast.44), channel_id=1, replica_groups=mesh['dp'=2,'fsdp'=4,'tensor'=4] {'dp'}, dimensions={0}, use_global_device_ids=true | all-gather | bytes 12288 | tf_op jit(solution)/shard_map/all_gather | solution.py:13
  292.9 4.3 %all-gather.6 = f32[2,1,1024]{2,1,0:T(1,128)S(1)} all-gather(f32[1,1,1024]{2,1,0:T(1,128)S(1)} %bitcast.43), channel_id=1, replica_groups=mesh['dp'=2,'fsdp'=4,'tensor'=4] {'dp'}, dimensions={0}, use_global_device_ids=true | all-gather | bytes 12288 | tf_op jit(solution)/shard_map/all_gather | solution.py:13
  297.2 4.3 %all-gather.4 = f32[2,1,1024]{2,1,0:T(1,128)S(1)} all-gather(f32[1,1,1024]{2,1,0:T(1,128)S(1)} %bitcast.42), channel_id=1, replica_groups=mesh['dp'=2,'fsdp'=4,'tensor'=4] {'dp'}, dimensions={0}, use_global_device_ids=true | all-gather | bytes 12288 | tf_op jit(solution)/shard_map/all_gather | solution.py:13
  301.6 0.1 subtract_add_fusion
  301.7 1.3 fusion.10
  303.0 0.7 select_reduce_fusion.1
  303.7 12.5 %all-reduce = (f32[]{:T(128)}, f32[]{:T(128)}, f32[]{:T(128)}, f32[]{:T(128)}) all-reduce(f32[]{:T(128)} %get-tuple-element.58, f32[]{:T(128)} %convert_reduce_fusion, f32[]{:T(128)} %select_reduce_fusion.1, f32[]{:T(128)} %get-tuple-element.51), channel_id=1, replica_groups=mesh['dp'=2,'fsdp'=4,'tensor'=4] {'dp','fsdp'}, use_global_device_ids=true, to_apply=%region_16.17 | all-reduce | flops 4 | bytes 32 | tf_op jit(solution)/shard_map/psum | solution.py:114
  320.1 0.6 pad_maximum_fusion
  (19 shorter events, 0.1 us)
Async XLA Ops:
  7.2 50.8 %all-gather.11.cloned.1.call-start = ((), (), s32[]{:S(2)}) async-start(), calls=%async_computation | async-start | bytes 2621440 | tf_op jit(solution)/shard_map/all_gather | solution.py:79
  7.9 111.4 %all-gather.13.cloned.1.call-start = ((), (), s32[]{:S(2)}) async-start(), calls=%async_computation.1 | async-start | bytes 6291456 | tf_op jit(solution)/shard_map/all_gather | solution.py:91
  63.5 161.4 %all-gather.15.cloned.1.call-start = ((), (), s32[]{:S(2)}) async-start(), calls=%async_computation.2 | async-start | bytes 20561920 | tf_op jit(solution)/shard_map/all_gather | solution.py:95
  63.6 6.4 %copy-start.4 = (f32[1,128]{1,0:T(1,128)S(1)}, f32[1,128]{1,0:T(1,128)}, u32[]{:S(2)}) copy-start(f32[1,128]{1,0:T(1,128)} %param.16) | copy-start | bytes 1540
  63.6 23.8 %copy-start.1 = (s32[1,512]{1,0:T(1,128)S(1)}, s32[1,512]{1,0:T(1,128)}, u32[]{:S(2)}) copy-start(s32[1,512]{1,0:T(1,128)} %param.12) | copy-start | bytes 6148
  264.3 37.4 %copy-start.2 = (f32[1,512]{1,0:T(1,128)S(1)}, f32[1,512]{1,0:T(1,128)}, u32[]{:S(2)}) copy-start(f32[1,512]{1,0:T(1,128)} %param.15) | copy-start | bytes 6148
  264.3 37.4 %copy-start.3 = (f32[1,512]{1,0:T(1,128)S(1)}, f32[1,512]{1,0:T(1,128)}, u32[]{:S(2)}) copy-start(f32[1,512]{1,0:T(1,128)} %param.14) | copy-start | bytes 6148
  301.7 19.0 %copy-start = (f32[512]{0:T(512)}, f32[512]{0:T(512)S(1)}, u32[]{:S(2)}) copy-start(f32[512]{0:T(512)S(1)} %get-tuple-element.55) | copy-start | bytes 6148
Sparse Core Ops, SparseCore 0:
  9.5 48.3 all-gather.10
  63.7 55.5 all-gather.12
  120.9 104.0 all-gather.14
where the time goes:
time: 328 us; the launch traced here: 327 us
  waiting for transfers between devices  169 us (52%)
  blocking collectives  92.7 us (28%)
  matrix products  23.4 us (7%)
  between operations  19.1 us (6%)
  other arithmetic  17.5 us (5%)
  local copies, waits for them, and re-layouts  5.08 us (2%)
    all_gather x1, waiting for transfers between devices, shards(): lax.all_gather(own_cols, 'fsdp', axis=0, tiled=True)  106 us
    all_gather x1, waiting for transfers between devices, shards(): lax.all_gather(hidden, 'tensor', axis=1, tiled=True)  35.7 us
    all_gather x1, waiting for transfers between devices, shards(): pair_rows = lax.all_gather(normed, 'dp', axis=0, tiled=True)  27.3 us
    dot_general x1, matrix products, shards(): jnp.dot(pair_rows, lax.all_gather(own_cols, 'fsdp', axis=0, tiled=True),...  23.4 us
    all_gather x4, blocking collectives, combined_all(): pieces = jax.tree.map(lambda part: lax.all_gather(part, axis), value)  17.4 us
    psum x1, blocking collectives, vocab_stats(): lax.psum((exp_sum, exp_square, picked), 'tensor')  15.5 us
    all_gather x1, blocking collectives, shards(): lax.all_gather(norm_gain, 'tensor', axis=0, tiled=True)  13.6 us
    psum x1, blocking collectives, shards(): lax.psum((jnp.sum(live_mask), jnp.sum(token_loss), jnp.sum(kl_part), jnp....  12.5 us
  transfers between devices with their start and end apart: 3, of which 3 were waited for; matrix products, arithmetic and copies ran while one was open for 2% of the time, Pallas kernels for 0%

commit v1 on v0

v1 whole, which is shorter than its diff:
```python
import functools

import jax
import jax.numpy as jnp
from jax import lax
from jax.experimental import pallas as pl
from jax.experimental.pallas import tpu as pltpu
from jax.sharding import PartitionSpec as P

MESH = pl.DeviceIdType.MESH
clip_eps = 0.2
kl_coef = 0.2
log_limit = 10.0
norm_eps = 1e-06
LANES = 128
LOW = -1e30


def token_terms(new_logp, old_logp, advantages, ref_logp, live_mask, prob_square):
    shift = new_logp - old_logp
    prob_ratio = jnp.exp(jnp.clip(shift, -log_limit, log_limit))
    clipped = jnp.clip(prob_ratio, 1.0 - clip_eps, 1.0 + clip_eps)
    plain_term = prob_ratio * advantages
    bounded_term = clipped * advantages
    surrogate = jnp.minimum(plain_term, bounded_term)
    ref_gap = ref_logp - new_logp
    gap_clip = jnp.clip(ref_gap, -log_limit, log_limit)
    gap_exp = jnp.exp(gap_clip)
    kl_term = gap_exp - gap_clip - 1.0
    token_loss = live_mask * (kl_coef * kl_term - surrogate)
    gap_part = jnp.where(jnp.abs(ref_gap) < log_limit, kl_coef * (1.0 - gap_exp), 0.0)
    active = (plain_term <= bounded_term) & (jnp.abs(shift) < log_limit)
    grad_coef = live_mask * (gap_part - jnp.where(active, plain_term, 0.0))
    grad_square = grad_coef * grad_coef * (prob_square - 2.0 * jnp.exp(new_logp) + 1.0)
    return (token_loss, live_mask * kl_term, grad_square)


class Config:
    def __init__(self, mesh, tok, dz, kr, vt):
        self.dp, self.fs, self.tz = (mesh.shape[a] for a in ("dp", "fsdp", "tensor"))
        self.groups = self.fs // 2
        self.tok, self.dz, self.kr, self.vt = tok, dz, kr, vt
        self.dim = dz * self.tz
        self.full_tiles = vt // LANES
        tiles = -(-vt // LANES)
        self.half_tiles = -(-tiles // (self.groups * self.dp))
        self.half_cols = self.half_tiles * LANES
        self.block_cols = self.half_cols * self.dp
        self.pad_cols = self.block_cols * self.groups
        self.steps = 8
        self.rows = tok // self.steps
        self.chunk = 256 if self.half_cols % 256 == 0 else LANES
        self.wsteps = self.half_cols // self.chunk
        self.resp = self.dp * self.fs


def kernel(
    c,
    hid, w_any, tail_any, pack_in, ids_in, old_in, adv_in, len_in, row_in,
    logp_out, loss_out, sum_out,
    x_buf, n_buf, w_own, w_full, packs, ids_all, rel, m_buf, l_buf, q_buf, p_buf,
    row_buf, roll, s_out, s_in, t_out, t_in,
    load_sem, x_sem, own_sem, tok_recv, y_send, right_send, left_send,
    wy_send, wy_recv, wx_send, wx_recv, core_send, core_recv,
    ids_send, ids_recv, pack_send, pack_recv, roll_send, roll_recv,
    st_send, st_recv, tot_send, tot_recv,
):
    G, Z, DP, F = c.groups, c.tz, c.dp, c.fs
    x = lax.axis_index("dp")
    f = lax.axis_index("fsdp")
    z = lax.axis_index("tensor")
    g, core = f // 2, f % 2
    partner = (x, g * 2 + (1 - core), z)
    me_resp = x * F + f
    pending = []

    def dev_g(gi):
        return (x, gi * 2 + core, z)

    def dev_x(xi):
        return (xi, f, z)

    def dev_z(zi):
        return (x, f, zi)

    def group(d):
        return lax.rem(g + d, G)

    def remote(src, dst, ss, rs, dev):
        return pltpu.make_async_remote_copy(
            src_ref=src, dst_ref=dst, send_sem=ss, recv_sem=rs, device_id=dev, device_id_type=MESH
        )

    def send(src, dst, ss, rs, dev, cond=None):
        copy = remote(src, dst, ss, rs, dev)
        if cond is None:
            copy.start()
        else:
            pl.when(cond)(copy.start)
        pending.append((cond, copy))

    def arrive(dst, rs, cond=None):
        copy = remote(dst, dst, rs, rs, partner)
        if cond is None:
            copy.wait_recv()
        else:
            pl.when(cond)(copy.wait_recv)

    main_cols = c.full_tiles * LANES
    loads = [
        pltpu.make_async_copy(
            w_any.at[:, pl.ds(0, main_cols)], w_own.at[:, pl.ds(0, main_cols)], load_sem.at[0]
        )
    ]
    if main_cols < c.vt:
        loads.append(
            pltpu.make_async_copy(tail_any, w_own.at[:, pl.ds(main_cols, LANES)], load_sem.at[1])
        )
    for copy in loads:
        copy.start()
    zcols = pl.ds(pl.multiple_of(z * c.dz, c.dz), c.dz)
    own_x = pltpu.make_async_copy(hid, x_buf.at[g, :, zcols], x_sem)
    own_x.start()
    filled = min(-(-c.vt // LANES) * LANES, c.pad_cols)
    if filled < c.pad_cols:
        w_own[:, filled:] = jnp.zeros((c.kr, c.pad_cols - filled), w_own.dtype)

    barrier = pltpu.get_barrier_semaphore()
    count = 0
    for dg in range(G):
        for s in range(Z):
            if dg or s:
                pl.semaphore_signal(
                    barrier, inc=1,
                    device_id=(x, group(dg) * 2 + core, lax.rem(z + s, Z)), device_id_type=MESH,
                )
                count += 1
    for dx in range(DP):
        for df in range(F):
            if dx or df % 2:
                pl.semaphore_signal(
                    barrier, inc=1,
                    device_id=(lax.rem(x + dx, DP), lax.rem(f + df, F), z), device_id_type=MESH,
                )
                count += 1
    pl.semaphore_wait(barrier, count)

    def piece(gi, q, zi):
        return x_buf.at[
            gi, pl.ds(q * c.rows, c.rows), pl.ds(pl.multiple_of(zi * c.dz, c.dz), c.dz)
        ]

    def hid_piece(q):
        return hid.at[pl.ds(q * c.rows, c.rows), :]

    def w_block(fi, h, j):
        return w_full.at[
            pl.ds(pl.multiple_of(fi * c.kr, c.kr), c.kr),
            pl.ds(pl.multiple_of(h * c.half_cols + j * c.chunk, c.chunk), c.chunk),
        ]

    def own_block(gi, h, j):
        start = gi * c.block_cols + h * c.half_cols + j * c.chunk
        return w_own.at[:, pl.ds(pl.multiple_of(start, c.chunk), c.chunk)]

    def y_tokens(q):
        for d in range(1, G):
            send(hid_piece(q), piece(g, q, z), y_send.at[d, q], tok_recv.at[g, q, z], dev_g(group(d)))

    def y_weights(j):
        for d in range(1, G):
            gi = group(d)
            send(own_block(gi, x, j), w_block(f, x, j), wy_send.at[d, j], wy_recv.at[g, j], dev_g(gi))

    def z_move(q, s):
        right_ok = z - s >= 0
        left_ok = z + s < Z
        zr = jnp.maximum(z - s, 0)
        zl = jnp.minimum(z + s, Z - 1)
        for d in range(G):
            gi = group(d)
            if s == 0:
                if d:
                    arrive(piece(gi, q, z), tok_recv.at[gi, q, z])
                src_r = src_l = hid_piece(q) if d == 0 else piece(gi, q, z)
            else:
                arrive(piece(gi, q, zr), tok_recv.at[gi, q, zr], right_ok)
                arrive(piece(gi, q, zl), tok_recv.at[gi, q, zl], left_ok)
                src_r, src_l = piece(gi, q, zr), piece(gi, q, zl)
            if s < Z - 1:
                send(src_r, piece(gi, q, zr), right_send.at[gi, q, zr], tok_recv.at[gi, q, zr],
                     dev_z(jnp.minimum(z + 1, Z - 1)), right_ok & (z + 1 < Z))
                send(src_l, piece(gi, q, zl), left_send.at[gi, q, zl], tok_recv.at[gi, q, zl],
                     dev_z(jnp.maximum(z - 1, 0)), left_ok & (z >= 1))

    def core_pass(src, fi, h, j):
        gi = fi // 2
        send(src, w_block(fi, h, j), core_send.at[gi, h, j], core_recv.at[gi, h, j], partner)

    for d in range(1, G):
        send(ids_in, ids_all.at[g], ids_send.at[d], ids_recv.at[g], dev_g(group(d)))
    for s in range(1, Z):
        send(pack_in, packs.at[z], pack_send.at[s], pack_recv.at[z], dev_z(lax.rem(z + s, Z)))
    y_tokens(0)
    z_first = 0

    for gi_init in range(G):
        m_buf[gi_init] = jnp.full(m_buf.shape[1:], LOW, jnp.float32)
        for ref in (l_buf, q_buf, p_buf):
            ref[gi_init] = jnp.zeros(ref.shape[1:], jnp.float32)
    packs[z] = pack_in[...]
    ids_all[g] = ids_in[...]
    for copy in loads:
        copy.wait()
    y_weights(0)
    own_copies = []
    for h in range(DP):
        start = pl.multiple_of(g * c.block_cols + h * c.half_cols, LANES)
        copy = pltpu.make_async_copy(
            w_own.at[:, pl.ds(start, c.half_cols)],
            w_full.at[pl.ds(pl.multiple_of(f * c.kr, c.kr), c.kr), pl.ds(h * c.half_cols, c.half_cols)],
            own_sem.at[h],
        )
        copy.start()
        own_copies.append(copy)

    def normalize(q):
        rows = pl.ds(q * c.rows, c.rows)
        for gi in range(G):
            values = x_buf[gi, rows, :].astype(jnp.float32)
            inv = lax.rsqrt(jnp.sum(values * values, axis=1, keepdims=True) / c.dim + norm_eps)
            for zi in range(Z):
                gain = packs[zi, 0:1, 0:c.dz]
                part = values[:, zi * c.dz : (zi + 1) * c.dz]
                n_buf[gi, rows, zi * c.dz : (zi + 1) * c.dz] = (part * inv * gain).astype(jnp.bfloat16)

    lane = lax.broadcasted_iota(jnp.int32, (1, LANES), 1)

    def unit(q, j):
        rows = pl.ds(pl.multiple_of(q * c.rows, c.rows), c.rows)
        for h in range(DP):
            off = h * c.half_cols + j * c.chunk
            cols = pl.ds(pl.multiple_of(off, c.chunk), c.chunk)
            tokens = jnp.concatenate([n_buf[gi, rows, :] for gi in range(G)], axis=0)
            logits = jnp.dot(tokens, w_full[:, cols], preferred_element_type=jnp.float32)
            valid = c.vt - g * c.block_cols - off
            for gi in range(G):
                part = logits[gi * c.rows : (gi + 1) * c.rows]
                place = rel[gi, rows, :] - off
                parts = []
                picked = p_buf[gi, rows, :]
                for t in range(c.chunk // LANES):
                    col = part[:, t * LANES : (t + 1) * LANES]
                    picked = picked + jnp.where(place == t * LANES, col, 0.0)
                    parts.append(jnp.where(lane + t * LANES < valid, col, LOW))
                p_buf[gi, rows, :] = picked
                before = m_buf[gi, rows, :]
                top = before
                for col in parts:
                    top = jnp.maximum(top, col)
                scale = jnp.exp(before - top)
                total = l_buf[gi, rows, :] * scale
                square = q_buf[gi, rows, :] * (scale * scale)
                for col in parts:
                    e = jnp.exp(col - top)
                    total = total + e
                    square = square + e * e
                m_buf[gi, rows, :] = top
                l_buf[gi, rows, :] = total
                q_buf[gi, rows, :] = square

    for i in range(c.steps + Z - 1):
        if i + 1 < c.steps:
            y_tokens(i + 1)
        if i + 1 < c.wsteps:
            y_weights(i + 1)
        if i < c.wsteps:
            for h in range(DP):
                core_pass(own_block(g, h, i), f, h, i)
        if i < c.steps:
            z_move(i, 0)
        if 0 <= i - 1 < c.wsteps:
            j = i - 1
            for d in range(1, G):
                gi = group(d)
                fi = gi * 2 + core
                arrive(w_block(fi, x, j), wy_recv.at[gi, j])
                for dx in range(1, DP):
                    xi = lax.rem(x + dx, DP)
                    send(w_block(fi, x, j), w_block(fi, x, j), wx_send.at[gi, dx, j],
                         wx_recv.at[gi, x, j], dev_x(xi))
                core_pass(w_block(fi, x, j), fi, x, j)
        for s in range(1, Z - 1):
            if 0 <= i - s < c.steps:
                z_move(i - s, s)
        if 0 <= i - 2 < c.wsteps:
            j = i - 2
            for d in range(1, G):
                gi = group(d)
                fi = gi * 2 + core
                for dx in range(1, DP):
                    xi = lax.rem(x + dx, DP)
                    arrive(w_block(fi, xi, j), wx_recv.at[gi, xi, j])
                    core_pass(w_block(fi, xi, j), fi, xi, j)
        if i == 1:
            for s in range(1, Z):
                zi = lax.rem(z + s, Z)
                arrive(packs.at[zi], pack_recv.at[zi])
            row_buf[...] = sum(packs[zi, :, c.dz :] for zi in range(Z))
            for d in range(1, G):
                arrive(ids_all.at[group(d)], ids_recv.at[group(d)])
            base = z * c.vt + g * c.block_cols
            for gi in range(G):
                spread = jnp.broadcast_to(ids_all[gi, 0:1, :], (LANES, c.tok))
                rel[gi] = spread.T.astype(jnp.int32) - base - lane
            own_x.wait()
            for copy in own_copies:
                copy.wait()
        if i == 2:
            for dx in range(DP):
                for df in range(F):
                    if dx or df:
                        xi, fi = lax.rem(x + dx, DP), lax.rem(f + df, F)
                        send(row_buf, roll.at[me_resp], roll_send.at[dx, df], roll_recv.at[me_resp],
                             (xi, fi, z))
        q = i - (Z - 1)
        if q >= 0:
            if q < c.wsteps:
                for gi in range(G):
                    for h in range(DP):
                        arrive(w_block(gi * 2 + 1 - core, h, q), core_recv.at[gi, h, q])
                if q:
                    pl.loop(0, q)(lambda qq, q=q: unit(qq, q))
            z_move(q, Z - 1)
            normalize(q)
            pl.loop(0, min(q + 1, c.wsteps))(lambda j, q=q: unit(q, j))

    for gi in range(G):
        m_t = m_buf[gi].T
        top = jnp.max(m_t, axis=0, keepdims=True)
        scale = jnp.exp(m_t - top)
        total = jnp.sum(l_buf[gi].T * scale, axis=0, keepdims=True)
        square = jnp.sum(q_buf[gi].T * (scale * scale), axis=0, keepdims=True)
        picked = jnp.sum(p_buf[gi].T, axis=0, keepdims=True)
        s_out[gi] = jnp.concatenate([top, total, square, picked, jnp.zeros((4, c.tok), jnp.float32)], axis=0)
    for s in range(Z - 1, -1, -1):
        for d in range(G):
            if s or d:
                gi, zi = group(d), lax.rem(z + s, Z)
                send(s_out.at[gi], s_in.at[g, z], st_send.at[d, s], st_recv.at[g, z],
                     (x, gi * 2 + core, zi))
    s_in[g, z] = s_out[g]

    roll[me_resp] = row_buf[...]
    for dx in range(DP):
        for df in range(F):
            if dx or df:
                r = lax.rem(x + dx, DP) * F + lax.rem(f + df, F)
                arrive(roll.at[r], roll_recv.at[r])
    ref = jnp.zeros((1, c.tok), jnp.float32)
    for r in range(c.resp):
        ref = ref + jnp.where(row_in[0] == r, roll[r, 0:1, :], 0.0)
    position = lax.broadcasted_iota(jnp.int32, (1, c.tok), 1)
    live = jnp.where(position < len_in[0], 1.0, 0.0)

    for s in range(Z):
        for d in range(G):
            if s or d:
                gi, zi = group(d), lax.rem(z + s, Z)
                arrive(s_in.at[gi, zi], st_recv.at[gi, zi])
    every = [(gi, zi) for gi in range(G) for zi in range(Z)]
    top = s_in[0, 0, 0:1, :]
    for gi, zi in every[1:]:
        top = jnp.maximum(top, s_in[gi, zi, 0:1, :])
    total = square = picked = jnp.zeros((1, c.tok), jnp.float32)
    for gi, zi in every:
        scale = jnp.exp(s_in[gi, zi, 0:1, :] - top)
        total = total + s_in[gi, zi, 1:2, :] * scale
        square = square + s_in[gi, zi, 2:3, :] * (scale * scale)
        picked = picked + s_in[gi, zi, 3:4, :]
    new_logp = picked - top - jnp.log(total)
    prob_square = square / (total * total)
    token_loss, kl_part, grad_part = token_terms(
        new_logp, old_in[...], adv_in[...], ref, live, prob_square
    )
    sums = [jnp.sum(v, axis=1, keepdims=True) for v in (live, token_loss, kl_part, grad_part)]
    t_out[...] = jnp.concatenate(
        [jnp.broadcast_to(v, (1, LANES)) for v in sums] + [jnp.zeros((4, LANES), jnp.float32)], axis=0
    )
    for dx in range(DP):
        for df in range(F):
            if dx or df:
                xi, fi = lax.rem(x + dx, DP), lax.rem(f + df, F)
                send(t_out, t_in.at[me_resp], tot_send.at[dx, df], tot_recv.at[me_resp], (xi, fi, z))
    t_in[me_resp] = t_out[...]
    logp_out[...] = new_logp
    loss_out[...] = token_loss
    for dx in range(DP):
        for df in range(F):
            if dx or df:
                r = lax.rem(x + dx, DP) * F + lax.rem(f + df, F)
                arrive(t_in.at[r], tot_recv.at[r])
    totals = sum(t_in[r] for r in range(c.resp))
    count = totals[0:1]
    sum_out[...] = jnp.concatenate(
        [totals[1:2] / count, totals[2:3] / count, jnp.sqrt(totals[3:4] / count), jnp.zeros((5, LANES), jnp.float32)],
        axis=0,
    )
    for cond, copy in pending:
        if cond is None:
            copy.wait_send()
        else:
            pl.when(cond)(copy.wait_send)


def shards(c_of, hidden, norm_gain, head_weight, token_ids, lengths, old_logp, advantages, rollout_logp, rollout_row):
    c = c_of(hidden.shape[0], hidden.shape[1], head_weight.shape[0], head_weight.shape[1])
    G, Z, DP, F = c.groups, c.tz, c.dp, c.fs
    z = lax.axis_index("tensor")
    main_cols = c.full_tiles * LANES
    tail = jnp.pad(head_weight[:, main_cols:], ((0, 0), (0, LANES - (c.vt - main_cols))))
    part = rollout_logp.shape[1]
    row = lax.dynamic_update_slice(jnp.zeros((1, c.tok), jnp.float32), rollout_logp, (0, z * part))
    pack = jnp.broadcast_to(
        jnp.concatenate([norm_gain.astype(jnp.float32)[None, :], row], axis=1), (8, c.dz + c.tok)
    )
    ids = jnp.broadcast_to(token_ids.astype(jnp.float32), (8, c.tok))
    vmem = pl.BlockSpec(memory_space=pltpu.VMEM)
    smem = pl.BlockSpec(memory_space=pltpu.SMEM)
    hbm = pl.BlockSpec(memory_space=pl.ANY)
    dma = lambda *shape: pltpu.SemaphoreType.DMA(shape)
    f32 = jnp.float32
    lanes = lambda dtype: pltpu.VMEM((G, c.tok, LANES), dtype)
    Q, J = c.steps, c.wsteps
    new_logp, token_loss, summary = pl.pallas_call(
        functools.partial(kernel, c),
        out_shape=(
            jax.ShapeDtypeStruct((1, c.tok), f32),
            jax.ShapeDtypeStruct((1, c.tok), f32),
            jax.ShapeDtypeStruct((8, LANES), f32),
        ),
        in_specs=[vmem, hbm, hbm, vmem, vmem, vmem, vmem, smem, smem],
        out_specs=(vmem, vmem, vmem),
        scratch_shapes=[
            pltpu.VMEM((G, c.tok, c.dim), jnp.bfloat16),
            pltpu.VMEM((G, c.tok, c.dim), jnp.bfloat16),
            pltpu.VMEM((c.kr, c.pad_cols), jnp.bfloat16),
            pltpu.VMEM((c.dim, c.block_cols), jnp.bfloat16),
            pltpu.VMEM((Z, 8, c.dz + c.tok), f32),
            pltpu.VMEM((G, 8, c.tok), f32),
            lanes(jnp.int32), lanes(f32), lanes(f32), lanes(f32), lanes(f32),
            pltpu.VMEM((8, c.tok), f32),
            pltpu.VMEM((c.resp, 8, c.tok), f32),
            pltpu.VMEM((G, 8, c.tok), f32),
            pltpu.VMEM((G, Z, 8, c.tok), f32),
            pltpu.VMEM((8, LANES), f32),
            pltpu.VMEM((c.resp, 8, LANES), f32),
            dma(2), pltpu.SemaphoreType.DMA, dma(DP), dma(G, Q, Z), dma(G, Q), dma(G, Q, Z), dma(G, Q, Z),
            dma(G, J), dma(G, J), dma(G, DP, J), dma(G, DP, J), dma(G, DP, J), dma(G, DP, J),
            dma(G), dma(G), dma(Z), dma(Z), dma(DP, F), dma(c.resp),
            dma(G, Z), dma(G, Z), dma(DP, F), dma(c.resp),
        ],
        compiler_params=pltpu.CompilerParams(
            collective_id=0, has_side_effects=True, vmem_limit_bytes=64 * 1024 * 1024 - 65536
        ),
    )(hidden, head_weight, tail, pack, ids, old_logp, advantages, lengths, rollout_row)
    return (new_logp, token_loss, summary[:3, 0])


def solution(mesh):
    rows = ("dp", "fsdp")
    in_specs = (
        P(rows, "tensor"), P("tensor"), P("fsdp", "tensor"), P(rows, None), P(rows),
        P(rows, None), P(rows, None), P(rows, "tensor"), P(rows),
    )
    out_specs = (P(rows, None), P(rows, None), P())
    return jax.shard_map(
        functools.partial(shards, functools.partial(Config, mesh)),
        mesh=mesh, in_specs=in_specs, out_specs=out_specs, check_vma=False,
    )
```

time: 328 us -> 130 us (0.40)
  waiting for transfers between devices: 169 us -> 0 us
  Pallas kernels: 0 us -> 109 us
  blocking collectives: 92.7 us -> 0 us
  matrix products: 23.4 us -> 0 us
  other arithmetic: 17.5 us -> 0.01 us
  between operations: 19.1 us -> 1.99 us
  local copies, waits for them, and re-layouts: 5.08 us -> 18.5 us
    all_gather x3 -> x0, waiting for transfers between devices: 169 us -> none  [the longest x1 106 us: shards(): lax.all_gather(own_cols, 'fsdp', axis=0, tiled=True)]
    pallas_call x0 -> x1, Pallas kernels: none -> 109 us  [shards(): pl.pallas_call(functools.partial(kernel, c), out_shape=(jax.ShapeDtypeStr...]
    all_gather x8 -> x0, blocking collectives: 53 us -> none  [the longest x4 17.4 us: combined_all(): pieces = jax.tree.map(lambda part: lax.all_gather(part, axis), value)]
    psum x2 -> x0, blocking collectives: 28 us -> none  [the longest x1 15.5 us: vocab_stats(): lax.psum((exp_sum, exp_square, picked), 'tensor')]
    dot_general x1 -> x0, matrix products: 23.4 us -> none  [shards(): jnp.dot(pair_rows, lax.all_gather(own_cols, 'fsdp', axis=0, tiled=True),...]
    unnamed x11 -> x9, local copies, waits for them, and re-layouts: 0.71 us -> 14.3 us
    reduce_sum x5 -> x0, other arithmetic: 13.3 us -> none  [the longest x1 8.68 us: exp_sums(): return (jnp.sum(shifted, axis=1), jnp.sum(shifted * shifted, axis=1))]
    pmax x1 -> x0, blocking collectives: 11.7 us -> none  [vocab_stats(): row_max = lax.pmax(local_max, 'tensor')]
  transfers between devices with their start and end apart: 3 -> 0, of which waited for: 3 -> 0; matrix products, arithmetic and copies ran while one was open for 2% -> 0% of each run, Pallas kernels for 0% -> 0%
where the time goes in v1:
time: 130 us
  Pallas kernels  109 us (84%)
  local copies, waits for them, and re-layouts  18.5 us (14%)
  between operations  1.99 us (2%)
    pallas_call x1, Pallas kernels, shards(): pl.pallas_call(functools.partial(kernel, c), out_shape=(jax.ShapeDtypeStr...  109 us
    unnamed x9, local copies, waits for them, and re-layouts  14.3 us

profile of v1, /device:TPU:0, one launch (start us, length us, event | category | flops | bytes accessed | tf_op | source)
XLA Modules:
  0.0 129.5 jit_solution(13317054902834897793)
XLA Ops:
  0.6 0.0 copy-start.2
  0.6 0.0 copy-start.1
  0.7 0.0 copy-start
  0.7 11.8 %copy.15.w_any = bf16[512,8032]{1,0:T(8,128)(2,1)} copy(bf16[512,8032]{0,1:T(8,128)(2,1)} %param.11) | data formatting | bytes 16449536 | tf_op args[2]
  12.5 0.9 slice.8
  13.4 0.7 pad.4.tail_any
  14.1 0.0 copy-done.2
  14.1 0.0 copy-done.1
  14.1 0.6 broadcast_in_dim.27.pack_in
  14.7 0.0 copy-done
  14.8 0.6 broadcast_in_dim.29.ids_in
  16.7 109.0 %shard_map.112 = (f32[1,512]{1,0:T(1,128)}, f32[1,512]{1,0:T(1,128)}, f32[8,128]{1,0:T(8,128)}) custom-call(bf16[512,512]{1,0:T(8,128)(2,1)} %hid.1, bf16[512,8032]{1,0:T(8,128)(2,1)} %copy.15.w_any, bf16[512,128]{1,0:T(8,128)(2,1)} %pad.4.tail_any, f32[8,1024]{1,0:T(8,128)} %broadcast_in_dim.27.pack_in, f32[8,512]{1,0:T(8,128)} %broadcast_in_dim.29.ids_in, ...), custom_call_target="tpu_custom_call" | custom-call | tf_op jit(solution)/shard_map/pallas_call | solution.py:435
  125.7 1.3 %slice_reduce_fusion = f32[3]{0:T(128)} fusion(f32[8,128]{1,0:T(8,128)} %get-tuple-element.8), kind=kLoop, calls=%fused_computation.1 | loop fusion | bytes 24 | tf_op jit(solution)/shard_map/slice | solution.py:467
  127.0 1.3 copy.21
  128.3 1.3 copy.22
  (5 shorter events, 0.0 us)
Async XLA Ops:
  0.6 13.5 %copy-start.2 = (f32[1,128]{1,0:T(1,128)S(1)}, f32[1,128]{1,0:T(1,128)}, u32[]{:S(2)}) copy-start(f32[1,128]{1,0:T(1,128)} %param.16) | copy-start | bytes 1540
  0.6 13.5 %copy-start.1 = (bf16[512]{0:T(512)(128)(2,1)S(1)}, bf16[512]{0:T(512)(128)(2,1)}, u32[]{:S(2)}) copy-start(bf16[512]{0:T(512)(128)(2,1)} %param.10) | copy-start | bytes 3076
  0.7 14.1 %copy-start = (s32[1,512]{1,0:T(1,128)S(1)}, s32[1,512]{1,0:T(1,128)}, u32[]{:S(2)}) copy-start(s32[1,512]{1,0:T(1,128)} %param.12) | copy-start | bytes 6148

commit v2 on v1

--- a/solution.py
+++ b/solution.py
@@ -41,7 +41,6 @@
         self.groups = self.fs // 2
         self.tok, self.dz, self.kr, self.vt = tok, dz, kr, vt
         self.dim = dz * self.tz
-        self.full_tiles = vt // LANES
         tiles = -(-vt // LANES)
         self.half_tiles = -(-tiles // (self.groups * self.dp))
         self.half_cols = self.half_tiles * LANES
@@ -51,13 +50,16 @@
         self.rows = tok // self.steps
         self.chunk = 256 if self.half_cols % 256 == 0 else LANES
         self.wsteps = self.half_cols // self.chunk
+        self.pairs = self.steps // 2
+        self.pair_rows = 2 * self.rows
         self.resp = self.dp * self.fs
 
 
 def kernel(
     c,
-    hid, w_any, tail_any, pack_in, ids_in, old_in, adv_in, len_in, row_in,
-    logp_out, loss_out, sum_out,
+    hid, gain_in, w_any, id_in, roll_in, old_in, adv_in, len_in, row_in,
+    out,
+    pack_in, ids_in,
     x_buf, n_buf, w_own, w_full, packs, ids_all, rel, m_buf, l_buf, q_buf, p_buf,
     row_buf, roll, s_out, s_in, t_out, t_in,
     load_sem, x_sem, own_sem, tok_recv, y_send, right_send, left_send,
@@ -106,24 +108,21 @@
         else:
             pl.when(cond)(copy.wait_recv)
 
-    main_cols = c.full_tiles * LANES
-    loads = [
-        pltpu.make_async_copy(
-            w_any.at[:, pl.ds(0, main_cols)], w_own.at[:, pl.ds(0, main_cols)], load_sem.at[0]
-        )
-    ]
-    if main_cols < c.vt:
-        loads.append(
-            pltpu.make_async_copy(tail_any, w_own.at[:, pl.ds(main_cols, LANES)], load_sem.at[1])
-        )
-    for copy in loads:
-        copy.start()
+    load = pltpu.make_async_copy(w_any, w_own.at[pl.ds(0, c.vt), :], load_sem)
+    load.start()
     zcols = pl.ds(pl.multiple_of(z * c.dz, c.dz), c.dz)
     own_x = pltpu.make_async_copy(hid, x_buf.at[g, :, zcols], x_sem)
     own_x.start()
-    filled = min(-(-c.vt // LANES) * LANES, c.pad_cols)
-    if filled < c.pad_cols:
-        w_own[:, filled:] = jnp.zeros((c.kr, c.pad_cols - filled), w_own.dtype)
+    if c.vt < c.pad_cols:
+        w_own[c.vt :, :] = jnp.zeros((c.pad_cols - c.vt, c.kr), w_own.dtype)
+    part = roll_in.shape[1]
+    pack_in[:, : c.dz] = jnp.broadcast_to(gain_in[...].astype(jnp.float32), (8, c.dz))
+    pack_in[:, c.dz :] = jnp.zeros((8, c.tok), jnp.float32)
+    for zi in range(Z):
+        @pl.when(z == zi)
+        def _(zi=zi):
+            pack_in[:, c.dz + zi * part : c.dz + (zi + 1) * part] = jnp.broadcast_to(roll_in[...], (8, part))
+    ids_in[...] = jnp.broadcast_to(id_in[...].astype(jnp.float32), (8, c.tok))
 
     barrier = pltpu.get_barrier_semaphore()
     count = 0
@@ -155,13 +154,13 @@
 
     def w_block(fi, h, j):
         return w_full.at[
+            pl.ds(pl.multiple_of(h * c.half_cols + j * c.chunk, c.chunk), c.chunk),
             pl.ds(pl.multiple_of(fi * c.kr, c.kr), c.kr),
-            pl.ds(pl.multiple_of(h * c.half_cols + j * c.chunk, c.chunk), c.chunk),
         ]
 
     def own_block(gi, h, j):
         start = gi * c.block_cols + h * c.half_cols + j * c.chunk
-        return w_own.at[:, pl.ds(pl.multiple_of(start, c.chunk), c.chunk)]
+        return w_own.at[pl.ds(pl.multiple_of(start, c.chunk), c.chunk), :]
 
     def y_tokens(q):
         for d in range(1, G):
@@ -202,23 +201,20 @@
     for s in range(1, Z):
         send(pack_in, packs.at[z], pack_send.at[s], pack_recv.at[z], dev_z(lax.rem(z + s, Z)))
     y_tokens(0)
-    z_first = 0
-
-    for gi_init in range(G):
-        m_buf[gi_init] = jnp.full(m_buf.shape[1:], LOW, jnp.float32)
-        for ref in (l_buf, q_buf, p_buf):
-            ref[gi_init] = jnp.zeros(ref.shape[1:], jnp.float32)
+
+    m_buf[...] = jnp.full(m_buf.shape, LOW, jnp.float32)
+    for ref in (l_buf, q_buf, p_buf):
+        ref[...] = jnp.zeros(ref.shape, jnp.float32)
     packs[z] = pack_in[...]
     ids_all[g] = ids_in[...]
-    for copy in loads:
-        copy.wait()
+    load.wait()
     y_weights(0)
     own_copies = []
     for h in range(DP):
         start = pl.multiple_of(g * c.block_cols + h * c.half_cols, LANES)
         copy = pltpu.make_async_copy(
-            w_own.at[:, pl.ds(start, c.half_cols)],
-            w_full.at[pl.ds(pl.multiple_of(f * c.kr, c.kr), c.kr), pl.ds(h * c.half_cols, c.half_cols)],
+            w_own.at[pl.ds(start, c.half_cols), :],
+            w_full.at[pl.ds(h * c.half_cols, c.half_cols), pl.ds(pl.multiple_of(f * c.kr, c.kr), c.kr)],
             own_sem.at[h],
         )
         copy.start()
@@ -234,40 +230,30 @@
                 part = values[:, zi * c.dz : (zi + 1) * c.dz]
                 n_buf[gi, rows, zi * c.dz : (zi + 1) * c.dz] = (part * inv * gain).astype(jnp.bfloat16)
 
-    lane = lax.broadcasted_iota(jnp.int32, (1, LANES), 1)
-
-    def unit(q, j):
-        rows = pl.ds(pl.multiple_of(q * c.rows, c.rows), c.rows)
+    def unit(p, start, size):
+        rows = pl.ds(pl.multiple_of(p * c.pair_rows, c.pair_rows), c.pair_rows)
+        width = G * c.pair_rows
         for h in range(DP):
-            off = h * c.half_cols + j * c.chunk
-            cols = pl.ds(pl.multiple_of(off, c.chunk), c.chunk)
+            off = h * c.half_cols + start
+            cols = pl.ds(pl.multiple_of(off, c.chunk), size)
             tokens = jnp.concatenate([n_buf[gi, rows, :] for gi in range(G)], axis=0)
-            logits = jnp.dot(tokens, w_full[:, cols], preferred_element_type=jnp.float32)
+            logits = lax.dot_general(
+                w_full[cols, :], tokens, (((1,), (1,)), ((), ())), preferred_element_type=jnp.float32
+            ).reshape(size // 8, 8, width)
             valid = c.vt - g * c.block_cols - off
-            for gi in range(G):
-                part = logits[gi * c.rows : (gi + 1) * c.rows]
-                place = rel[gi, rows, :] - off
-                parts = []
-                picked = p_buf[gi, rows, :]
-                for t in range(c.chunk // LANES):
-                    col = part[:, t * LANES : (t + 1) * LANES]
-                    picked = picked + jnp.where(place == t * LANES, col, 0.0)
-                    parts.append(jnp.where(lane + t * LANES < valid, col, LOW))
-                p_buf[gi, rows, :] = picked
-                before = m_buf[gi, rows, :]
-                top = before
-                for col in parts:
-                    top = jnp.maximum(top, col)
-                scale = jnp.exp(before - top)
-                total = l_buf[gi, rows, :] * scale
-                square = q_buf[gi, rows, :] * (scale * scale)
-                for col in parts:
-                    e = jnp.exp(col - top)
-                    total = total + e
-                    square = square + e * e
-                m_buf[gi, rows, :] = top
-                l_buf[gi, rows, :] = total
-                q_buf[gi, rows, :] = square
+            place = rel[p] - off
+            index = lax.broadcasted_iota(jnp.int32, (size // 8, 8, 1), 0) * 8 + lax.broadcasted_iota(
+                jnp.int32, (size // 8, 8, 1), 1
+            )
+            p_buf[p] = p_buf[p] + jnp.sum(jnp.where(index == place[None], logits, 0.0), axis=0)
+            logits = jnp.where(index < valid, logits, LOW)
+            before = m_buf[p]
+            top = jnp.maximum(before, jnp.max(logits, axis=0))
+            scale = jnp.exp(before - top)
+            e = jnp.exp(logits - top[None])
+            m_buf[p] = top
+            l_buf[p] = l_buf[p] * scale + jnp.sum(e, axis=0)
+            q_buf[p] = q_buf[p] * (scale * scale) + jnp.sum(e * e, axis=0)
 
     for i in range(c.steps + Z - 1):
         if i + 1 < c.steps:
@@ -310,9 +296,10 @@
             for d in range(1, G):
                 arrive(ids_all.at[group(d)], ids_recv.at[group(d)])
             base = z * c.vt + g * c.block_cols
-            for gi in range(G):
-                spread = jnp.broadcast_to(ids_all[gi, 0:1, :], (LANES, c.tok))
-                rel[gi] = spread.T.astype(jnp.int32) - base - lane
+            for p in range(c.pairs):
+                for gi in range(G):
+                    ids = ids_all[gi, :, p * c.pair_rows : (p + 1) * c.pair_rows]
+                    rel[p, :, gi * c.pair_rows : (gi + 1) * c.pair_rows] = ids.astype(jnp.int32) - base
             own_x.wait()
             for copy in own_copies:
                 copy.wait()
@@ -329,20 +316,31 @@
                 for gi in range(G):
                     for h in range(DP):
                         arrive(w_block(gi * 2 + 1 - core, h, q), core_recv.at[gi, h, q])
-                if q:
-                    pl.loop(0, q)(lambda qq, q=q: unit(qq, q))
+                p = q // 2
+                if q % 2 or q == c.wsteps - 1:
+                    first = q - q % 2
+                    if p:
+                        pl.loop(0, p)(lambda pp, q=q, first=first: unit(pp, first * c.chunk, (q + 1 - first) * c.chunk))
             z_move(q, Z - 1)
             normalize(q)
-            pl.loop(0, min(q + 1, c.wsteps))(lambda j, q=q: unit(q, j))
-
-    for gi in range(G):
-        m_t = m_buf[gi].T
-        top = jnp.max(m_t, axis=0, keepdims=True)
-        scale = jnp.exp(m_t - top)
-        total = jnp.sum(l_buf[gi].T * scale, axis=0, keepdims=True)
-        square = jnp.sum(q_buf[gi].T * (scale * scale), axis=0, keepdims=True)
-        picked = jnp.sum(p_buf[gi].T, axis=0, keepdims=True)
-        s_out[gi] = jnp.concatenate([top, total, square, picked, jnp.zeros((4, c.tok), jnp.float32)], axis=0)
+            if q % 2:
+                ready = min(q + 1, c.wsteps)
+                span = min(2, ready)
+                pl.loop(0, ready // span)(lambda jj, q=q, span=span: unit(q // 2, jj * (span * c.chunk), span * c.chunk))
+
+    s_out[...] = jnp.zeros(s_out.shape, jnp.float32)
+    for p in range(c.pairs):
+        m_p = m_buf[p]
+        top = jnp.max(m_p, axis=0, keepdims=True)
+        scale = jnp.exp(m_p - top)
+        total = jnp.sum(l_buf[p] * scale, axis=0, keepdims=True)
+        square = jnp.sum(q_buf[p] * (scale * scale), axis=0, keepdims=True)
+        picked = jnp.sum(p_buf[p], axis=0, keepdims=True)
+        for gi in range(G):
+            here = slice(gi * c.pair_rows, (gi + 1) * c.pair_rows)
+            there = slice(p * c.pair_rows, (p + 1) * c.pair_rows)
+            for k, value in enumerate((top, total, square, picked)):
+                s_out[gi, k : k + 1, there] = value[:, here]
     for s in range(Z - 1, -1, -1):
         for d in range(G):
             if s or d:
@@ -393,8 +391,8 @@
                 xi, fi = lax.rem(x + dx, DP), lax.rem(f + df, F)
                 send(t_out, t_in.at[me_resp], tot_send.at[dx, df], tot_recv.at[me_resp], (xi, fi, z))
     t_in[me_resp] = t_out[...]
-    logp_out[...] = new_logp
-    loss_out[...] = token_loss
+    out[0:1, :] = new_logp
+    out[1:2, :] = token_loss
     for dx in range(DP):
         for df in range(F):
             if dx or df:
@@ -402,10 +400,9 @@
                 arrive(t_in.at[r], tot_recv.at[r])
     totals = sum(t_in[r] for r in range(c.resp))
     count = totals[0:1]
-    sum_out[...] = jnp.concatenate(
-        [totals[1:2] / count, totals[2:3] / count, jnp.sqrt(totals[3:4] / count), jnp.zeros((5, LANES), jnp.float32)],
-        axis=0,
-    )
+    for k, value in enumerate((totals[1:2] / count, totals[2:3] / count, jnp.sqrt(totals[3:4] / count))):
+        out[2 + k : 3 + k, :] = jnp.broadcast_to(value[:, 0:1], (1, c.tok))
+    out[5:8, :] = jnp.zeros((3, c.tok), jnp.float32)
     for cond, copy in pending:
         if cond is None:
             copy.wait_send()
@@ -416,36 +413,25 @@
 def shards(c_of, hidden, norm_gain, head_weight, token_ids, lengths, old_logp, advantages, rollout_logp, rollout_row):
     c = c_of(hidden.shape[0], hidden.shape[1], head_weight.shape[0], head_weight.shape[1])
     G, Z, DP, F = c.groups, c.tz, c.dp, c.fs
-    z = lax.axis_index("tensor")
-    main_cols = c.full_tiles * LANES
-    tail = jnp.pad(head_weight[:, main_cols:], ((0, 0), (0, LANES - (c.vt - main_cols))))
-    part = rollout_logp.shape[1]
-    row = lax.dynamic_update_slice(jnp.zeros((1, c.tok), jnp.float32), rollout_logp, (0, z * part))
-    pack = jnp.broadcast_to(
-        jnp.concatenate([norm_gain.astype(jnp.float32)[None, :], row], axis=1), (8, c.dz + c.tok)
-    )
-    ids = jnp.broadcast_to(token_ids.astype(jnp.float32), (8, c.tok))
     vmem = pl.BlockSpec(memory_space=pltpu.VMEM)
     smem = pl.BlockSpec(memory_space=pltpu.SMEM)
     hbm = pl.BlockSpec(memory_space=pl.ANY)
     dma = lambda *shape: pltpu.SemaphoreType.DMA(shape)
     f32 = jnp.float32
-    lanes = lambda dtype: pltpu.VMEM((G, c.tok, LANES), dtype)
+    lanes = lambda dtype: pltpu.VMEM((c.pairs, 8, G * c.pair_rows), dtype)
     Q, J = c.steps, c.wsteps
-    new_logp, token_loss, summary = pl.pallas_call(
+    out = pl.pallas_call(
         functools.partial(kernel, c),
-        out_shape=(
-            jax.ShapeDtypeStruct((1, c.tok), f32),
-            jax.ShapeDtypeStruct((1, c.tok), f32),
-            jax.ShapeDtypeStruct((8, LANES), f32),
-        ),
-        in_specs=[vmem, hbm, hbm, vmem, vmem, vmem, vmem, smem, smem],
-        out_specs=(vmem, vmem, vmem),
+        out_shape=jax.ShapeDtypeStruct((8, c.tok), f32),
+        in_specs=[vmem, vmem, hbm, vmem, vmem, vmem, vmem, smem, smem],
+        out_specs=vmem,
         scratch_shapes=[
+            pltpu.VMEM((8, c.dz + c.tok), f32),
+            pltpu.VMEM((8, c.tok), f32),
             pltpu.VMEM((G, c.tok, c.dim), jnp.bfloat16),
             pltpu.VMEM((G, c.tok, c.dim), jnp.bfloat16),
-            pltpu.VMEM((c.kr, c.pad_cols), jnp.bfloat16),
-            pltpu.VMEM((c.dim, c.block_cols), jnp.bfloat16),
+            pltpu.VMEM((c.pad_cols, c.kr), jnp.bfloat16),
+            pltpu.VMEM((c.block_cols, c.dim), jnp.bfloat16),
             pltpu.VMEM((Z, 8, c.dz + c.tok), f32),
             pltpu.VMEM((G, 8, c.tok), f32),
             lanes(jnp.int32), lanes(f32), lanes(f32), lanes(f32), lanes(f32),
@@ -455,7 +441,7 @@
             pltpu.VMEM((G, Z, 8, c.tok), f32),
             pltpu.VMEM((8, LANES), f32),
             pltpu.VMEM((c.resp, 8, LANES), f32),
-            dma(2), pltpu.SemaphoreType.DMA, dma(DP), dma(G, Q, Z), dma(G, Q), dma(G, Q, Z), dma(G, Q, Z),
+            pltpu.SemaphoreType.DMA, pltpu.SemaphoreType.DMA, dma(DP), dma(G, Q, Z), dma(G, Q), dma(G, Q, Z), dma(G, Q, Z),
             dma(G, J), dma(G, J), dma(G, DP, J), dma(G, DP, J), dma(G, DP, J), dma(G, DP, J),
             dma(G), dma(G), dma(Z), dma(Z), dma(DP, F), dma(c.resp),
             dma(G, Z), dma(G, Z), dma(DP, F), dma(c.resp),
@@ -463,8 +449,8 @@
         compiler_params=pltpu.CompilerParams(
             collective_id=0, has_side_effects=True, vmem_limit_bytes=64 * 1024 * 1024 - 65536
         ),
-    )(hidden, head_weight, tail, pack, ids, old_logp, advantages, lengths, rollout_row)
-    return (new_logp, token_loss, summary[:3, 0])
+    )(hidden, norm_gain[None, :], head_weight.T, token_ids, rollout_logp, old_logp, advantages, lengths, rollout_row)
+    return (out[0:1], out[1:2], out[2:5, 0])
 
 
 def solution(mesh):

time: 130 us -> 113 us (0.87)
  local copies, waits for them, and re-layouts: 18.5 us -> 3.95 us
  Pallas kernels: 109 us -> 107 us
    unnamed x9 -> x0, local copies, waits for them, and re-layouts: 14.3 us -> none
    pallas_call x1, Pallas kernels: 109 us -> 107 us  [shards(): pl.pallas_call(functools.partial(kernel, c), out_shape=jax.ShapeDtypeStru...]
where the time goes in v2:
time: 113 us
  Pallas kernels  107 us (95%)
  local copies, waits for them, and re-layouts  3.95 us (3%)
  between operations  1.94 us (2%)
    pallas_call x1, Pallas kernels, shards(): pl.pallas_call(functools.partial(kernel, c), out_shape=jax.ShapeDtypeStru...  107 us
    slice x2, local copies, waits for them, and re-layouts, shards(): return (out[0:1], out[1:2], out[2:5, 0])  2.69 us

profile of v2, /device:TPU:0, one launch (start us, length us, event | category | flops | bytes accessed | tf_op | source)
XLA Modules:
  0.0 112.9 jit_solution(7380379604846909821)
XLA Ops:
  0.6 1.3 %broadcast_in_dim.3.gain_in = bf16[1,512]{1,0:T(2,128)(2,1)} reshape(bf16[512]{0:T(512)(128)(2,1)} %param.10) | data formatting | bytes 2048 | tf_op jit(solution)/shard_map/broadcast_in_dim | solution.py:452
  3.2 107.0 %shard_map.112 = f32[8,512]{1,0:T(8,128)} custom-call(bf16[512,512]{1,0:T(8,128)(2,1)} %hid.1, bf16[1,512]{1,0:T(2,128)(2,1)} %broadcast_in_dim.3.gain_in, bf16[8032,512]{1,0:T(8,128)(2,1)} %bitcast.1, s32[1,512]{1,0:T(1,128)} %id_in.1, f32[1,128]{1,0:T(1,128)} %roll_in.1, f32[1,512]{1,0:T(1,128)} %old_in.1, f32[1,512]{1,0:T(1,128)} %adv_in.1, ...), custom_call_target="tpu_custom_call" | custom-call | tf_op jit(solution)/shard_map/pallas_call | solution.py:423
  110.2 1.4 %fusion = (f32[1,512]{1,0:T(1,128)}, f32[1,512]{1,0:T(1,128)}) fusion(f32[8,512]{1,0:T(8,128)} %shard_map.112), kind=kLoop, calls=%fused_computation.1 | loop fusion | bytes 8192 | tf_op jit(solution)/shard_map/slice | solution.py:453
  111.6 1.3 %slice_reduce_fusion = f32[3]{0:T(128)} fusion(f32[8,512]{1,0:T(8,128)} %shard_map.112), kind=kLoop, calls=%fused_computation | loop fusion | bytes 24 | tf_op jit(solution)/shard_map/slice | solution.py:453
